TPU v7x, 32 devices: a whole 2x2x4 slice. The times are simulated.
32 devices in a mesh: rep: 2 (over y), fsdp: 16 (over z, x, core).
Axes of the slice: x: 2, y: 2, z: 4, core: 2. Of those that a mesh axis runs over, the one named last changes fastest.
Arguments:
- tokens: bfloat16 [16384, 4096], P(('rep', 'fsdp')), may hold values from -6 to 6
- value_cot: bfloat16 [16384, 1024], P(('rep', 'fsdp')), may hold values from -6 to 6
- value_weight: bfloat16 [2, 4096, 1024], P('rep', 'fsdp'), may hold values from -0.09375 to 0.09375
- global_params: float32 [2097152], P('fsdp'), may hold values from -6 to 6
- local_params: float32 [2, 2097152], P('rep', 'fsdp'), may hold values from -6 to 6
- momentum: float32 [2097152], P('fsdp'), may hold values from -3 to 3
Outputs:
- token_grad: bfloat16 [16384, 4096], P(('rep', 'fsdp'))
- value_grad: float32 [2, 4096, 1024], P('rep', 'fsdp')
- new_global: float32 [2097152], P('fsdp')
- new_moment: float32 [2097152], P('fsdp')
All inputs are finite; a program needn't handle non-finite values.
Results may differ from a plain program's by a relative error of at most 0.001.
Values may be sent and summed in bfloat16 or wider, within the bound.
A program may use at most 128 MiB of HBM per device.

v0:
```python
import functools

import jax
import jax.numpy as jnp
from jax import lax
from jax.experimental import pallas as pl
from jax.experimental.pallas import tpu as pltpu
from jax.sharding import PartitionSpec as P

CORES = 2
COLS = 2
SCALE = 2.0 ** 8


def grad_term(tokens, columns):
    return lax.dot_general(
        tokens, columns, (((0,), (0,)), ((), ())), preferred_element_type=jnp.float32
    )


def acc_cut(extent, tile):
    return extent * 5 // (8 * tile) * tile


def pack(v):
    v = v * SCALE
    v = v * jnp.abs(v)
    return (v * jnp.abs(v)).astype(jnp.bfloat16)


def unpack(p):
    p = p.astype(jnp.float32)
    r = jnp.sqrt(jnp.sqrt(jnp.abs(p))) * (1.0 / SCALE)
    return jnp.where(p < 0, -r, r)


def kernel(groups, factor, x_ref, c_ref, w_ref, tg_ref, vg_ref,
           wbuf, xr, cr, acc_a, acc_b, sax, rax, saz, raz, sbz, rbz, sbx, rbx,
           rw, szr, szl, sx, sc, xs, xrs, cs, own_sem, axs, axr, azs, azr, bzs, bzr, bxs):
    nz = groups // (CORES * COLS)
    f = lax.axis_index("fsdp")
    core, x, z = lax.rem(f, CORES), lax.rem(f // CORES, COLS), f // (CORES * COLS)
    depth = w_ref.shape[0]
    cut = acc_cut(depth, 16)
    wide = acc_cut(c_ref.shape[1], 128)

    def ident(zz, xx, cc):
        return (zz * COLS + xx) * CORES + cc

    ox, oc = 1 - x, 1 - core
    xdev, cdev = ident(z, ox, core), ident(z, x, oc)
    rdev, ldev = ident(z + 1, x, core), ident(z - 1, x, core)
    has_r, has_l = z < nz - 1, z > 0

    def both(fn):
        pl.when(has_r)(lambda: fn(rdev))
        pl.when(has_l)(lambda: fn(ldev))

    barrier = pltpu.get_barrier_semaphore()

    def greet(dev):
        pl.semaphore_signal(barrier, inc=1, device_id={"fsdp": dev}, device_id_type=pl.DeviceIdType.MESH)

    own = pltpu.make_async_copy(w_ref, wbuf.at[f], own_sem)
    own.start()
    greet(xdev)
    greet(cdev)
    both(greet)
    pl.semaphore_wait(barrier, 2 + jnp.where(has_r, 1, 0) + jnp.where(has_l, 1, 0))

    def remote(src, dst, ssem, rsem, dev):
        return pltpu.make_async_remote_copy(
            src_ref=src, dst_ref=dst, send_sem=ssem, recv_sem=rsem,
            device_id={"fsdp": dev}, device_id_type=pl.DeviceIdType.MESH)

    cot = remote(c_ref, cr, cs.at[0], cs.at[1], cdev)
    cot.start()

    def xcopy(q):
        d = q * CORES + oc
        return remote(x_ref.at[:, pl.ds(pl.multiple_of(d * depth, depth), depth)], xr.at[q], xs.at[q], xrs.at[q], cdev)

    nq = nz * COLS

    @pl.loop(0, nq)
    def _(q):
        xcopy(q).start()

    own.wait()

    def piece(h, blk, ssem, dev):
        part = wbuf.at[blk, pl.ds(0, cut) if h == 0 else pl.ds(cut, depth - cut)]
        return remote(part, part, ssem.at[h, blk], rw.at[h, blk], dev)

    def right(h, blk):
        return piece(h, blk, szr, rdev)

    def left(h, blk):
        return piece(h, blk, szl, ldev)

    def across(h, blk):
        return piece(h, blk, sx, xdev)

    def core_way(h, blk):
        return piece(h, blk, sc, cdev)

    def send_z(h, blk):
        pl.when(has_r)(lambda: right(h, blk).start())
        pl.when(has_l)(lambda: left(h, blk).start())

    across(1, f).start()
    send_z(0, f)
    send_z(1, f)
    core_way(0, f).start()
    core_way(1, f).start()

    cot.wait_recv()

    @pl.loop(0, nq)
    def _(q):
        xcopy(q).wait_recv()

    def grad(zz, xx):
        q = zz * COLS + xx
        d = ident(zz, xx, core)
        cols = pl.ds(pl.multiple_of(d * depth, depth), depth)
        return grad_term(x_ref[:, cols], c_ref[...]) + grad_term(xr[q], cr[...])

    def ax(zz):
        return remote(sax.at[zz], rax.at[zz], axs.at[zz], axr.at[zz], xdev)

    @pl.loop(0, nz)
    def _(zz):
        g = grad(zz, ox)
        sax[zz] = pack(g[:, :wide])
        ax(zz).start()
        acc_b[zz, ox] = g[:, wide:]

    across(0, f).start()

    other = ident(z, ox, core)
    across(1, other).wait_recv()
    send_z(1, other)
    core_way(1, other).start()

    @pl.loop(0, nz)
    def _(zz):
        g = grad(zz, x)
        acc_a[zz] = g[:, :wide]
        acc_b[zz, x] = g[:, wide:]

    def hop(k):
        for h in range(2):
            for ok, zo, fwd, nxt in ((z - k >= 0, z - k, right, has_r), (z + k < nz, z + k, left, has_l)):
                @pl.when(ok)
                def _():
                    for xx in ((x,) if h == 0 else (x, ox)):
                        blk = ident(zo, xx, core)
                        fwd(h, blk).wait_recv()
                        pl.when(nxt)(lambda: fwd(h, blk).start())
                        if h == 0:
                            across(h, blk).start()
                        core_way(h, blk).start()

    def line(acc, sbuf, rbuf, ssem, rsem):
        def copy(way, zz):
            return remote(sbuf.at[zz], rbuf.at[way, zz], ssem.at[zz], rsem.at[way, zz], rdev if way == 0 else ldev)

        def step(s):
            late = nz - 1 - s
            for way, zz, ok, came in ((0, z + late, z <= s, has_l), (1, z - late, nz - 1 - z <= s, has_r)):
                @pl.when(jnp.logical_and(ok, came))
                def _():
                    copy(way, zz).wait_recv()
                    acc[zz] += unpack(rbuf[way, zz])

                if late:
                    @pl.when(ok)
                    def _():
                        sbuf[zz] = pack(acc[zz])
                        copy(way, zz).start()

        def drain():
            for zz in range(nz):
                pl.when(zz > z)(lambda: copy(0, zz).wait_send())
                pl.when(zz < z)(lambda: copy(1, zz).wait_send())

        return step, drain

    step_a, drain_a = line(acc_a, saz, raz, azs, azr)
    step_b, drain_b = line(acc_b, sbz, rbz, bzs, bzr)

    step_b(0)
    for s in range(1, nz):
        hop(s)
        step_b(s)
        if s == 1:
            @pl.loop(0, nz)
            def _(zz):
                ax(zz).wait_recv()
                acc_a[zz] += unpack(rax[zz])
        if s == nz - 1:
            bx = remote(sbx, rbx, bxs.at[0], bxs.at[1], xdev)
            sbx[...] = pack(acc_b[z, ox])
            bx.start()
        step_a(s - 1)

    for zo in range(nz):
        blk = ident(zo, ox, core)
        across(0, blk).wait_recv()
        core_way(0, blk).start()

    def project(d):
        tg_ref[:, pl.ds(pl.multiple_of(d * depth, depth), depth)] = lax.dot_general(
            c_ref[...], wbuf[d], (((1,), (1,)), ((), ())), preferred_element_type=jnp.float32
        ).astype(jnp.bfloat16)

    @pl.loop(0, nq)
    def _(q):
        project(q * CORES + core)

    step_a(nz - 1)
    vg_ref[:, :wide] = acc_a[z] * factor
    bx.wait_recv()
    vg_ref[:, wide:] = (acc_b[z, x] + unpack(rbx[...])) * factor

    @pl.loop(0, nq)
    def _(q):
        d = q * CORES + oc
        core_way(0, d).wait_recv()
        core_way(1, d).wait_recv()
        project(d)

    cot.wait_send()
    bx.wait_send()
    drain_a()
    drain_b()

    @pl.loop(0, nq)
    def _(q):
        xcopy(q).wait_send()
        d = q * CORES + core
        core_way(0, d).wait_send()
        core_way(1, d).wait_send()

    across(1, f).wait_send()

    @pl.loop(0, nz)
    def _(zz):
        ax(zz).wait_send()
        across(0, ident(zz, x, core)).wait_send()
        go_r = jnp.logical_and(zz <= z, has_r)
        go_l = jnp.logical_and(zz >= z, has_l)
        for h, xx in ((0, x), (1, x), (1, ox)):
            pl.when(go_r)(lambda: right(h, ident(zz, xx, core)).wait_send())
            pl.when(go_l)(lambda: left(h, ident(zz, xx, core)).wait_send())


def fused(tokens, value_cot, weight, groups, factor):
    nz = groups // (CORES * COLS)
    rows, wide = tokens.shape[0], value_cot.shape[1]
    depth = weight.shape[0]
    wa = acc_cut(wide, 128)
    wb = wide - wa
    bf, f32 = jnp.bfloat16, jnp.float32
    dma = pltpu.SemaphoreType.DMA
    vmem = pl.BlockSpec(memory_space=pltpu.VMEM)
    return pl.pallas_call(
        functools.partial(kernel, groups, factor),
        out_shape=(
            jax.ShapeDtypeStruct((rows, tokens.shape[1]), bf),
            jax.ShapeDtypeStruct((depth, wide), f32),
        ),
        in_specs=[vmem] * 3,
        out_specs=(vmem, vmem),
        scratch_shapes=[
            pltpu.VMEM((groups, depth, wide), bf),
            pltpu.VMEM((nz * COLS, rows, depth), bf),
            pltpu.VMEM((rows, wide), bf),
            pltpu.VMEM((nz, depth, wa), f32),
            pltpu.VMEM((nz, COLS, depth, wb), f32),
            pltpu.VMEM((nz, depth, wa), bf),
            pltpu.VMEM((nz, depth, wa), bf),
            pltpu.VMEM((nz, depth, wa), bf),
            pltpu.VMEM((2, nz, depth, wa), bf),
            pltpu.VMEM((nz, COLS, depth, wb), bf),
            pltpu.VMEM((2, nz, COLS, depth, wb), bf),
            pltpu.VMEM((depth, wb), bf),
            pltpu.VMEM((depth, wb), bf),
            dma((2, groups)), dma((2, groups)), dma((2, groups)), dma((2, groups)), dma((2, groups)),
            dma((nz * COLS,)), dma((nz * COLS,)), dma((2,)), dma,
            dma((nz,)), dma((nz,)), dma((nz,)), dma((2, nz)), dma((nz,)), dma((2, nz)), dma((2,)),
        ],
        compiler_params=pltpu.CompilerParams(
            collective_id=0, has_side_effects=True, vmem_limit_bytes=42 * 1024 * 1024
        ),
        cost_estimate=pl.CostEstimate(flops=80_000_000_000, bytes_accessed=20_000_000, transcendentals=0),
    )(tokens, value_cot, weight)


def shards(tokens, value_cot, value_weight, global_params, local_params, momentum):
    weight = value_weight[0]
    groups = lax.axis_size("fsdp")
    reps = lax.axis_size("rep")
    local = local_params[0]
    factor = 1.0 / float(tokens.shape[0] * groups) ** 0.5
    if reps == 2:
        totals = local + lax.ppermute(local, "rep", [(0, 1), (1, 0)])
    else:
        totals = lax.psum(local, "rep")
    depth = weight.shape[0]
    if depth % 128 == 0 and groups % (CORES * COLS) == 0 and groups > CORES * COLS:
        token_grad, value_grad = fused(tokens, value_cot, weight, groups, factor)
    else:
        token_grad = lax.dot_general(
            value_cot,
            lax.all_gather(weight, "fsdp", axis=0, tiled=True),
            (((1,), (1,)), ((), ())),
            preferred_element_type=jnp.float32,
        ).astype(jnp.bfloat16)
        value_grad = factor * lax.psum_scatter(
            grad_term(tokens, value_cot), "fsdp", scatter_dimension=0, tiled=True
        )
    pseudo = global_params - totals / reps
    new_moment = 0.9 * momentum + pseudo
    new_global = global_params - 0.7 * (pseudo + 0.9 * new_moment)
    return (token_grad, value_grad[None], new_global, new_moment)


def solution(mesh):
    in_specs = (
        P(("rep", "fsdp"), None),
        P(("rep", "fsdp"), None),
        P("rep", "fsdp", None),
        P("fsdp"),
        P("rep", "fsdp"),
        P("fsdp"),
    )
    out_specs = (P(("rep", "fsdp"), None), P("rep", "fsdp", None), P("fsdp"), P("fsdp"))
    return jax.shard_map(shards, mesh=mesh, in_specs=in_specs, out_specs=out_specs, check_vma=False)
```

profile of v0, /device:TPU:0, one launch (start us, length us, event | category | flops | bytes accessed | tf_op | source)
XLA Modules:
  0.0 92.2 jit_solution(14229369239859502334)
XLA Ops:
  0.6 3.1 %collective-permute-start = (f32[131072]{0:T(1024)}, f32[131072]{0:T(1024)S(1)}, u32[]{:S(2)}, u32[]{:S(2)}) collective-permute-start(f32[131072]{0:T(1024)} %bitcast.5), channel_id=1, source_target_pairs={{0,16},{16,0},{1,17},{17,1},{2,18},{18,2},{3,19},{19,3},{4,20},{20... | collective-permute-start | bytes 1572872 | tf_op jit(solution)/shard_map/ppermute | solution.py:308
  3.7 0.0 copy-start
  3.7 2.2 %copy-done = bf16[512,4096]{1,0:T(8,128)(2,1)S(1)} copy-done((bf16[512,4096]{1,0:T(8,128)(2,1)S(1)}, bf16[512,4096]{1,0:T(8,128)(2,1)}, u32[]{:S(2)}) %copy-start) | copy-done | bytes 4194328
  5.9 0.0 copy-start.1
  5.9 1.2 %copy-done.1 = bf16[512,1024]{1,0:T(8,128)(2,1)S(1)} copy-done((bf16[512,1024]{1,0:T(8,128)(2,1)S(1)}, bf16[512,1024]{1,0:T(8,128)(2,1)}, u32[]{:S(2)}) %copy-start.1) | copy-done | bytes 1048600
  7.1 0.0 copy-start.2
  7.1 1.0 %copy-done.2 = bf16[1,256,1024]{2,1,0:T(8,128)(2,1)S(1)} copy-done((bf16[1,256,1024]{2,1,0:T(8,128)(2,1)S(1)}, bf16[1,256,1024]{2,1,0:T(8,128)(2,1)}, u32[]{:S(2)}) %copy-start.2) | copy-done | bytes 524312
  8.1 0.0 copy-start.3
  8.2 0.0 copy-start.4
  8.2 0.0 copy-start.5
  8.2 79.9 %shard_map.93 = (bf16[512,4096]{1,0:T(8,128)(2,1)S(1)}, f32[256,1024]{1,0:T(8,128)S(1)}) custom-call(bf16[512,4096]{1,0:T(8,128)(2,1)S(1)} %copy-done, bf16[512,1024]{1,0:T(8,128)(2,1)S(1)} %copy-done.1, bf16[256,1024]{1,0:T(8,128)(2,1)S(1)} %bitcast.4), custom_call_target="tpu_custom_call" | custom-call | flops 80000000000 | bytes 20000000 | tf_op jit(solution)/shard_map/pallas_call | solution.py:268
  88.0 0.0 collective-permute-done
  88.0 0.0 copy-done.3
  88.1 0.0 copy-done.4
  88.1 0.0 copy-done.5
  88.1 1.1 %multiply_subtract_fusion = (f32[131072]{0:T(1024)}, f32[131072]{0:T(1024)}) fusion(f32[131072]{0:T(1024)S(1)} %copy-done.3, f32[131072]{0:T(1024)S(1)} %bitcast.6, f32[131072]{0:T(1024)S(1)} %collective-permute-done, f32[131072]{0:T(1024)S(1)} %copy-done.5), kind=kLoop, calls=%fused_computation | loop fusion | flops 1179648 | bytes 3145728 | tf_op jit(solution)/shard_map/sub | solution.py:326
  89.2 2.0 %copy.12 = bf16[512,4096]{1,0:T(8,128)(2,1)} copy(bf16[512,4096]{1,0:T(8,128)(2,1)S(1)} %get-tuple-element.14) | data formatting | bytes 8388608
  91.2 1.0 %copy.13 = f32[1,256,1024]{2,1,0:T(8,128)} copy(f32[1,256,1024]{2,1,0:T(8,128)S(1)} %bitcast.3) | data formatting | bytes 2097152
Async XLA Ops:
  0.6 87.4 %collective-permute-start = (f32[131072]{0:T(1024)}, f32[131072]{0:T(1024)S(1)}, u32[]{:S(2)}, u32[]{:S(2)}) collective-permute-start(f32[131072]{0:T(1024)} %bitcast.5), channel_id=1, source_target_pairs={{0,16},{16,0},{1,17},{17,1},{2,18},{18,2},{3,19},{19,3},{4,20},{20... | collective-permute-start | bytes 1572872 | tf_op jit(solution)/shard_map/ppermute | solution.py:308
  3.7 2.2 %copy-start = (bf16[512,4096]{1,0:T(8,128)(2,1)S(1)}, bf16[512,4096]{1,0:T(8,128)(2,1)}, u32[]{:S(2)}) copy-start(bf16[512,4096]{1,0:T(8,128)(2,1)} %x_ref.1) | copy-start | bytes 12582916
  5.9 1.2 %copy-start.1 = (bf16[512,1024]{1,0:T(8,128)(2,1)S(1)}, bf16[512,1024]{1,0:T(8,128)(2,1)}, u32[]{:S(2)}) copy-start(bf16[512,1024]{1,0:T(8,128)(2,1)} %c_ref.1) | copy-start | bytes 3145732
  7.1 1.0 %copy-start.2 = (bf16[1,256,1024]{2,1,0:T(8,128)(2,1)S(1)}, bf16[1,256,1024]{2,1,0:T(8,128)(2,1)}, u32[]{:S(2)}) copy-start(bf16[1,256,1024]{2,1,0:T(8,128)(2,1)} %param.8) | copy-start | bytes 1572868
  8.1 79.9 %copy-start.3 = (f32[131072]{0:T(1024)S(1)}, f32[131072]{0:T(1024)}, u32[]{:S(2)}) copy-start(f32[131072]{0:T(1024)} %param.9) | copy-start | bytes 1572868
  8.2 79.9 %copy-start.4 = (f32[1,131072]{1,0:T(1,128)S(1)}, f32[1,131072]{1,0:T(1,128)}, u32[]{:S(2)}) copy-start(f32[1,131072]{1,0:T(1,128)} %param.10) | copy-start | bytes 1572868
  8.2 79.9 %copy-start.5 = (f32[131072]{0:T(1024)S(1)}, f32[131072]{0:T(1024)}, u32[]{:S(2)}) copy-start(f32[131072]{0:T(1024)} %param.11) | copy-start | bytes 1572868
where the time goes:
time: 92.6 us; the launch traced here: 92.2 us
  Pallas kernels  79.9 us (86%)
  local copies, waits for them, and re-layouts  7.45 us (8%)
  starting transfers between devices  3.06 us (3%)
  other arithmetic  1.12 us (1%)
    pallas_call x1, Pallas kernels, fused(): pl.pallas_call(functools.partial(kernel, groups, factor), out_shape=(jax....  79.9 us
    unnamed x14, local copies, waits for them, and re-layouts  7.45 us
    ppermute x1, starting transfers between devices, shards(): totals = local + lax.ppermute(local, 'rep', [(0, 1), (1, 0)])  3.06 us
  transfers between devices with their start and end apart: 1, of which 0 were waited for; matrix products, arithmetic and copies ran while one was open for 0% of the time, Pallas kernels for 87%

commit v1 on v0

v1 whole, which is shorter than its diff:
```python
import functools

import jax
import jax.numpy as jnp
from jax import lax
from jax.experimental import pallas as pl
from jax.experimental.pallas import tpu as pltpu
from jax.sharding import PartitionSpec as P

CORES = 2
COLS = 2
SCALE = 2.0 ** 8


def grad_term(tokens, columns):
    return lax.dot_general(
        tokens, columns, (((0,), (0,)), ((), ())), preferred_element_type=jnp.float32
    )


def acc_cut(extent, tile):
    return extent * 5 // (8 * tile) * tile


def pack(v):
    v = v * SCALE
    v = v * jnp.abs(v)
    return (v * jnp.abs(v)).astype(jnp.bfloat16)


def unpack(p):
    p = p.astype(jnp.float32)
    r = jnp.sqrt(jnp.sqrt(jnp.abs(p))) * (1.0 / SCALE)
    return jnp.where(p < 0, -r, r)


def kernel(groups, reps, factor, x_hbm, c_hbm, w_hbm, g_hbm, l_hbm, m_hbm, tg_ref, vg_ref, ng_ref, nm_ref,
           wbuf, xb, cb, acc_a, acc_b, sax, rax, saz, raz, sbz, rbz, sbx, rbx, gb, lb, mb, lr,
           rw, szr, szl, sx, sc, xl, xs, xrs, cl, cs, own_sem, us, axs, axr, azs, azr, bzs, bzr, bxs):
    nz = groups // (CORES * COLS)
    f = lax.axis_index("fsdp")
    rep = lax.axis_index("rep")
    core, x, z = lax.rem(f, CORES), lax.rem(f // CORES, COLS), f // (CORES * COLS)
    rows, depth = x_hbm.shape[0], w_hbm.shape[0]
    cut = acc_cut(depth, 16)
    wide = acc_cut(c_hbm.shape[1], 128)

    def ident(zz, xx, cc):
        return (zz * COLS + xx) * CORES + cc

    ox, oc = 1 - x, 1 - core
    xdev, cdev = ident(z, ox, core), ident(z, x, oc)
    rdev, ldev = ident(z + 1, x, core), ident(z - 1, x, core)
    has_r, has_l = z < nz - 1, z > 0
    low = z < nz // 2

    def far(i):
        down = nz - 1 - i
        down = jnp.where(down <= z, down - 1, down)
        up = jnp.where(i >= z, i + 1, i)
        return jnp.where(i == nz - 1, z, jnp.where(low, down, up))

    def columns(d):
        return pl.ds(pl.multiple_of(d * depth, depth), depth)

    def xload(q):
        return pltpu.make_async_copy(x_hbm.at[:, columns(q * CORES + core)], xb.at[q, pl.ds(0, rows)], xl.at[q])

    def order(i):
        return jnp.where(i < nz, far(i) * COLS + ox, far(i - nz) * COLS + x)

    nq = nz * COLS
    own = pltpu.make_async_copy(w_hbm, wbuf.at[f], own_sem)
    own.start()
    cload = pltpu.make_async_copy(c_hbm, cb.at[pl.ds(0, rows)], cl)
    cload.start()

    barrier = pltpu.get_barrier_semaphore()

    def greet(dev):
        pl.semaphore_signal(barrier, inc=1, device_id={"fsdp": dev}, device_id_type=pl.DeviceIdType.MESH)

    greet(xdev)
    greet(cdev)
    pl.when(has_r)(lambda: greet(rdev))
    pl.when(has_l)(lambda: greet(ldev))
    pl.semaphore_signal(barrier, inc=1, device_id={"rep": 1 - rep}, device_id_type=pl.DeviceIdType.MESH)

    @pl.loop(0, nq)
    def _(i):
        xload(order(i)).start()

    loads = [pltpu.make_async_copy(src, dst, us.at[n]) for n, (src, dst) in enumerate(((g_hbm, gb), (l_hbm, lb), (m_hbm, mb)))]
    for load in loads:
        load.start()
    pl.semaphore_wait(barrier, 3 + jnp.where(has_r, 1, 0) + jnp.where(has_l, 1, 0))

    def remote(src, dst, ssem, rsem, dev):
        return pltpu.make_async_remote_copy(
            src_ref=src, dst_ref=dst, send_sem=ssem, recv_sem=rsem,
            device_id={"fsdp": dev}, device_id_type=pl.DeviceIdType.MESH)

    def piece(h, blk, ssem, dev):
        part = wbuf.at[blk, pl.ds(0, cut) if h == 0 else pl.ds(cut, depth - cut)]
        return remote(part, part, ssem.at[h, blk], rw.at[h, blk], dev)

    def right(h, blk):
        return piece(h, blk, szr, rdev)

    def left(h, blk):
        return piece(h, blk, szl, ldev)

    def across(h, blk):
        return piece(h, blk, sx, xdev)

    def core_way(h, blk):
        return piece(h, blk, sc, cdev)

    def send_z(h, blk):
        pl.when(has_r)(lambda: right(h, blk).start())
        pl.when(has_l)(lambda: left(h, blk).start())

    def xcopy(q):
        return remote(x_hbm.at[:, columns(q * CORES + oc)], xb.at[q, pl.ds(rows, rows)], xs.at[q], xrs.at[q], cdev)

    cot = remote(c_hbm, cb.at[pl.ds(rows, rows)], cs.at[0], cs.at[1], cdev)
    swap = pltpu.make_async_remote_copy(
        src_ref=l_hbm, dst_ref=lr, send_sem=us.at[3], recv_sem=us.at[4],
        device_id={"rep": 1 - rep}, device_id_type=pl.DeviceIdType.MESH)

    own.wait()
    across(1, f).start()
    send_z(0, f)
    across(0, f).start()
    send_z(1, f)
    cot.start()
    xcopy(order(0)).start()
    core_way(0, f).start()
    core_way(1, f).start()

    @pl.loop(1, nq)
    def _(i):
        xcopy(order(i)).start()

    swap.start()

    def project(d):
        tg_ref[:, columns(d)] = lax.dot_general(
            cb[pl.ds(0, rows)], wbuf[d], (((1,), (1,)), ((), ())), preferred_element_type=jnp.float32
        ).astype(jnp.bfloat16)

    cload.wait()
    project(f)
    core_way(0, cdev).wait_recv()
    core_way(1, cdev).wait_recv()
    project(cdev)
    cot.wait_recv()

    def grad(zz, xx):
        q = zz * COLS + xx
        xload(q).wait()
        xcopy(q).wait_recv()
        return grad_term(xb[q], cb[...])

    def ax(zz):
        return remote(sax.at[zz], rax.at[zz], axs.at[zz], axr.at[zz], xdev)

    other = ident(z, ox, core)

    @pl.loop(0, nz)
    def _(i):
        zz = far(i)
        g = grad(zz, ox)
        sax[zz] = pack(g[:, :wide])
        ax(zz).start()
        acc_b[zz, ox] = g[:, wide:]

        @pl.when(i == 1)
        def _():
            across(1, other).wait_recv()
            send_z(1, other)
            core_way(1, other).start()

    def hop(k, h, xx):
        for ok, zo, fwd, nxt in ((z - k >= 0, z - k, right, has_r), (z + k < nz, z + k, left, has_l)):
            @pl.when(ok)
            def _():
                blk = ident(zo, xx, core)
                fwd(h, blk).wait_recv()
                pl.when(nxt)(lambda: fwd(h, blk).start())
                if h == 0:
                    across(h, blk).start()
                core_way(h, blk).start()

    @pl.loop(0, nz)
    def _(i):
        zz = far(i)
        g = grad(zz, x)
        acc_a[zz] = g[:, :wide]
        acc_b[zz, x] = g[:, wide:]

        @pl.when(i == 1)
        def _():
            hop(1, 0, x)

    def line(acc, sbuf, rbuf, ssem, rsem):
        def copy(way, zz):
            return remote(sbuf.at[zz], rbuf.at[way, zz], ssem.at[zz], rsem.at[way, zz], rdev if way == 0 else ldev)

        def step(s):
            late = nz - 1 - s
            for way, zz, ok, came in ((0, z + late, z <= s, has_l), (1, z - late, nz - 1 - z <= s, has_r)):
                @pl.when(jnp.logical_and(ok, came))
                def _():
                    copy(way, zz).wait_recv()
                    acc[zz] += unpack(rbuf[way, zz])

                if late:
                    @pl.when(ok)
                    def _():
                        sbuf[zz] = pack(acc[zz])
                        copy(way, zz).start()

        def drain():
            for zz in range(nz):
                pl.when(zz > z)(lambda: copy(0, zz).wait_send())
                pl.when(zz < z)(lambda: copy(1, zz).wait_send())

        return step, drain

    step_a, drain_a = line(acc_a, saz, raz, azs, azr)
    step_b, drain_b = line(acc_b, sbz, rbz, bzs, bzr)

    def add_ax(i):
        zz = far(i)
        ax(zz).wait_recv()
        acc_a[zz] += unpack(rax[zz])

    def land(h, d):
        core_way(h, d).wait_recv()

    def column(k):
        for ok, zo in ((z - k >= 0, z - k), (z + k < nz, z + k)):
            @pl.when(ok)
            def _():
                project(ident(zo, x, core))
                d = ident(zo, x, oc)
                land(0, d)
                land(1, d)
                project(d)

    def late(zo):
        blk = ident(zo, ox, core)
        across(0, blk).wait_recv()
        core_way(0, blk).start()
        project(blk)

    def late_other(zo):
        d = ident(zo, ox, oc)
        land(0, d)
        land(1, d)
        project(d)

    step_b(0)
    hop(1, 1, x)
    hop(1, 1, ox)
    add_ax(0)
    step_a(0)
    late(z)
    late_other(z)

    swap.wait_recv()
    for load in loads:
        load.wait()
    pseudo = gb[...] - (lb[...] + lr[...]) / reps
    moment = 0.9 * mb[...] + pseudo
    nm_ref[...] = moment
    ng_ref[...] = gb[...] - 0.7 * (pseudo + 0.9 * moment)

    for s in range(1, nz):
        if s + 1 < nz:
            column(s)
            hop(s + 1, 0, x)
        else:
            column(s)
            late(far(nz - 2))
            if nz > 3:
                late(far(nz - 3))
            late_other(far(nz - 2))
        step_b(s)
        if s + 1 < nz:
            hop(s + 1, 1, x)
            hop(s + 1, 1, ox)
            add_ax(s)
            step_a(s)

    bx = remote(sbx, rbx, bxs.at[0], bxs.at[1], xdev)
    sbx[...] = pack(acc_b[z, ox])
    bx.start()
    if nz > 3:
        late_other(far(nz - 3))
    for i in range(max(nz - 4, 0), -1, -1):
        late(far(i))
        late_other(far(i))
    add_ax(nz - 1)
    step_a(nz - 1)
    vg_ref[:, :wide] = acc_a[z] * factor
    bx.wait_recv()
    vg_ref[:, wide:] = (acc_b[z, x] + unpack(rbx[...])) * factor

    cot.wait_send()
    bx.wait_send()
    swap.wait_send()
    drain_a()
    drain_b()

    @pl.loop(0, nq)
    def _(q):
        xcopy(q).wait_send()
        d = q * CORES + core
        core_way(0, d).wait_send()
        core_way(1, d).wait_send()

    across(1, f).wait_send()

    @pl.loop(0, nz)
    def _(zz):
        ax(zz).wait_send()
        across(0, ident(zz, x, core)).wait_send()
        go_r = jnp.logical_and(zz <= z, has_r)
        go_l = jnp.logical_and(zz >= z, has_l)
        for h, xx in ((0, x), (1, x), (1, ox)):
            pl.when(go_r)(lambda: right(h, ident(zz, xx, core)).wait_send())
            pl.when(go_l)(lambda: left(h, ident(zz, xx, core)).wait_send())


def flush(*refs):
    count = len(refs) // 2
    sems = refs[-1]
    copies = [pltpu.make_async_copy(refs[n], refs[count + n], sems.at[n]) for n in range(count)]
    for copy in copies:
        copy.start()
    for copy in copies:
        copy.wait()


def fused(tokens, value_cot, weight, outer, local, momentum, groups, reps, factor):
    nz = groups // (CORES * COLS)
    rows, wide = tokens.shape[0], value_cot.shape[1]
    depth = weight.shape[0]
    wa = acc_cut(wide, 128)
    wb = wide - wa
    bf, f32 = jnp.bfloat16, jnp.float32
    dma = pltpu.SemaphoreType.DMA
    hbm = pl.BlockSpec(memory_space=pltpu.HBM)
    vmem = pl.BlockSpec(memory_space=pltpu.VMEM)
    frag = outer.shape
    kinds = (((rows, tokens.shape[1]), bf), ((depth, wide), f32), (frag, f32), (frag, f32))
    operands = [pltpu.with_memory_space_constraint(v, pltpu.HBM) for v in (tokens, value_cot, weight, outer, local, momentum)]
    results = pl.pallas_call(
        functools.partial(kernel, groups, reps, factor),
        out_shape=tuple(pltpu.VMEM(shape, kind) for shape, kind in kinds),
        in_specs=[hbm] * 6,
        out_specs=(vmem,) * 4,
        scratch_shapes=[
            pltpu.VMEM((groups, depth, wide), bf),
            pltpu.VMEM((nz * COLS, 2 * rows, depth), bf),
            pltpu.VMEM((2 * rows, wide), bf),
            pltpu.VMEM((nz, depth, wa), f32),
            pltpu.VMEM((nz, COLS, depth, wb), f32),
            pltpu.VMEM((nz, depth, wa), bf),
            pltpu.VMEM((nz, depth, wa), bf),
            pltpu.VMEM((nz, depth, wa), bf),
            pltpu.VMEM((2, nz, depth, wa), bf),
            pltpu.VMEM((nz, COLS, depth, wb), bf),
            pltpu.VMEM((2, nz, COLS, depth, wb), bf),
            pltpu.VMEM((depth, wb), bf),
            pltpu.VMEM((depth, wb), bf),
            pltpu.VMEM(frag, f32), pltpu.VMEM(frag, f32), pltpu.VMEM(frag, f32), pltpu.VMEM(frag, f32),
            dma((2, groups)), dma((2, groups)), dma((2, groups)), dma((2, groups)), dma((2, groups)),
            dma((nz * COLS,)), dma((nz * COLS,)), dma((nz * COLS,)), dma, dma((2,)), dma, dma((5,)),
            dma((nz,)), dma((nz,)), dma((nz,)), dma((2, nz)), dma((nz,)), dma((2, nz)), dma((2,)),
        ],
        compiler_params=pltpu.CompilerParams(
            collective_id=0, has_side_effects=True, vmem_limit_bytes=48 * 1024 * 1024
        ),
        cost_estimate=pl.CostEstimate(flops=80_000_000_000, bytes_accessed=20_000_000, transcendentals=0),
    )(*operands)
    return pl.pallas_call(
        flush,
        out_shape=tuple(pltpu.HBM(shape, kind) for shape, kind in kinds),
        in_specs=[vmem] * 4,
        out_specs=(hbm,) * 4,
        scratch_shapes=[dma((4,))],
        compiler_params=pltpu.CompilerParams(vmem_limit_bytes=1024 * 1024),
        cost_estimate=pl.CostEstimate(flops=1_000_000, bytes_accessed=12_000_000, transcendentals=0),
    )(*[pltpu.with_memory_space_constraint(v, pltpu.VMEM) for v in results])


def shards(tokens, value_cot, value_weight, global_params, local_params, momentum):
    weight = value_weight[0]
    groups = lax.axis_size("fsdp")
    reps = lax.axis_size("rep")
    local = local_params[0]
    factor = 1.0 / float(tokens.shape[0] * groups) ** 0.5
    depth = weight.shape[0]
    if reps == 2 and depth % 128 == 0 and groups % (CORES * COLS) == 0 and groups > CORES * COLS:
        flat = global_params.shape
        tall = (flat[0] // 128, 128)
        token_grad, value_grad, new_global, new_moment = fused(
            tokens, value_cot, weight, global_params.reshape(tall), local.reshape(tall), momentum.reshape(tall),
            groups, reps, factor,
        )
        return (token_grad, value_grad[None], new_global.reshape(flat), new_moment.reshape(flat))
    totals = lax.psum(local, "rep")
    token_grad = lax.dot_general(
        value_cot,
        lax.all_gather(weight, "fsdp", axis=0, tiled=True),
        (((1,), (1,)), ((), ())),
        preferred_element_type=jnp.float32,
    ).astype(jnp.bfloat16)
    value_grad = factor * lax.psum_scatter(
        grad_term(tokens, value_cot), "fsdp", scatter_dimension=0, tiled=True
    )
    pseudo = global_params - totals / reps
    new_moment = 0.9 * momentum + pseudo
    new_global = global_params - 0.7 * (pseudo + 0.9 * new_moment)
    return (token_grad, value_grad[None], new_global, new_moment)


def solution(mesh):
    in_specs = (
        P(("rep", "fsdp"), None),
        P(("rep", "fsdp"), None),
        P("rep", "fsdp", None),
        P("fsdp"),
        P("rep", "fsdp"),
        P("fsdp"),
    )
    out_specs = (P(("rep", "fsdp"), None), P("rep", "fsdp", None), P("fsdp"), P("fsdp"))
    return jax.shard_map(shards, mesh=mesh, in_specs=in_specs, out_specs=out_specs, check_vma=False)
```

time: 92.6 us -> 75.8 us (0.82)
  local copies, waits for them, and re-layouts: 7.45 us -> 0 us
  Pallas kernels: 79.9 us -> 74.8 us
  starting transfers between devices: 3.06 us -> 0 us
  other arithmetic: 1.12 us -> 0 us
    unnamed x14 -> x0, local copies, waits for them, and re-layouts: 7.45 us -> none
    pallas_call x1 -> x2, Pallas kernels: 79.9 us -> 74.8 us  [the longest x1 72.2 us: fused(): pl.pallas_call(functools.partial(kernel, groups, reps, factor), out_shape...]
    ppermute x1 -> x0, starting transfers between devices: 3.06 us -> none  [shards(): totals = local + lax.ppermute(local, 'rep', [(0, 1), (1, 0)])]
    sub x1 -> x0, other arithmetic: 1.12 us -> none  [shards(): new_global = global_params - 0.7 * (pseudo + 0.9 * new_moment)]
  transfers between devices with their start and end apart: 1 -> 0, of which waited for: 0 -> 0; matrix products, arithmetic and copies ran while one was open for 0% -> 0% of each run, Pallas kernels for 87% -> 0%
where the time goes in v1:
time: 75.8 us; the launch traced here: 75.6 us
  Pallas kernels  74.8 us (99%)
  between operations  0.8 us (1%)
    pallas_call x1, Pallas kernels, fused(): pl.pallas_call(functools.partial(kernel, groups, reps, factor), out_shape...  72.2 us
    pallas_call x1, Pallas kernels, fused(): pl.pallas_call(flush, out_shape=tuple((pltpu.HBM(shape, kind) for shape,...  2.68 us

profile of v1, /device:TPU:0, one launch (start us, length us, event | category | flops | bytes accessed | tf_op | source)
XLA Modules:
  0.0 75.6 jit_solution(7277036950873608767)
XLA Ops:
  0.6 72.2 %shard_map.93 = (bf16[512,4096]{1,0:T(8,128)(2,1)S(1)}, f32[256,1024]{1,0:T(8,128)S(1)}, f32[1024,128]{1,0:T(8,128)S(1)}, f32[1024,128]{1,0:T(8,128)S(1)}) custom-call(bf16[512,4096]{1,0:T(8,128)(2,1)} %x_hbm.1, bf16[512,1024]{1,0:T(8,128)(2,1)} %c_hbm.1, bf16[256,1024]{1,0:T(8,128)(2,1)} %bitcast.8, f32[1024,128]{1,0:T(8,128)} %bitcast.9, ...), custom_call_target="tpu_custom_call" | custom-call | flops 80000000000 | bytes 20000000 | tf_op jit(solution)/shard_map/pallas_call | solution.py:360
  72.8 2.7 %shard_map.94 = (bf16[512,4096]{1,0:T(8,128)(2,1)}, f32[256,1024]{1,0:T(8,128)}, f32[1024,128]{1,0:T(8,128)}, f32[1024,128]{1,0:T(8,128)}) custom-call(bf16[512,4096]{1,0:T(8,128)(2,1)S(1)} %get-tuple-element.12.refs_0_, f32[256,1024]{1,0:T(8,128)S(1)} %get-tuple-element.13.refs_1_, f32[1024,128]{1,0:T(8,128)S(1)} %get-tuple-element.14.refs_2_, ...), custom_call_target="tpu_custom_call" | custom-call | flops 1000000 | bytes 12000000 | tf_op jit(solution)/shard_map/pallas_call | solution.py:389
